TPU v7x, 32 devices: a whole 2x2x4 slice. The times are simulated.
32 devices in a mesh: clump: 8 (over z, y), grp: 4 (over x, core).
Axes of the slice: x: 2, y: 2, z: 4, core: 2. Of those that a mesh axis runs over, the one named last changes fastest.
Arguments:
- flux: float32 [32, 1024, 64], P(('clump', 'grp')), may hold values from -6 to 6
- patch_pft: int32 [32, 1024], P(('clump', 'grp')), may hold values from 0 to 15
- patch_wt: float32 [32, 1024], P(('clump', 'grp')), may hold values from 0.2 to 2
- patch_col: int32 [32, 1024], P(('clump', 'grp')), may hold values from 0 to 511, never falling along the last dimension, each value on 1 to 4 neighbouring positions
- col_wt: float32 [32, 512], P(('clump', 'grp')), may hold values from 0.2 to 2
- col_lu: int32 [32, 512], P(('clump', 'grp')), may hold values from 0 to 255, never falling along the last dimension, each value on 1 to 4 neighbouring positions
- lu_wt: float32 [32, 256], P(('clump', 'grp')), may hold values from 0.2 to 2
- lu_grid: int32 [32, 256], P(('clump', 'grp')), may hold values from 0 to 127, never falling along the last dimension, each value on 1 to 4 neighbouring positions
- cell_target: int32 [32, 128], P(('clump', 'grp')), may hold values from 0 to 4095, as said below
- patch_count: int32 [32], P(('clump', 'grp')), may hold values from 64 to 1024
- pft_scale: float32 [16, 64], replicated, may hold values from 0.3 to 3
- cpl_frac: float32 [4096], P(('clump', 'grp')), may hold values from 0.2 to 0.9
- cpl_field: float32 [4096, 64], P(('clump', 'grp')), may hold values from -6 to 6
Outputs:
- grid_merged: float32 [4096, 64], P(('clump', 'grp'))
- anomaly: float32 [32, 1024, 64], P(('clump', 'grp'))
Inputs may be any that keep to these rules, and one draw needn't show every extreme that they name: `patch_col`: within each device's row the column numbers never fall, and each column holds 1 to 4 patch slots. `col_lu`: within each device's row the landunit numbers never fall, and each landunit holds 1 to 4 columns. `lu_grid`: within each device's row the gridcell numbers never fall, and each gridcell holds 1 to 4 landunits. `cell_target`: all devices' entries together are a permutation of 0 to 4095; the coupler owner of an entry q is q // 128, and each device's 128 gridcells go to 16 owners, exactly 8 to each.
All inputs are finite; a program needn't handle non-finite values.
Results may differ from a plain program's by a relative error of at most 0.0003.
Values sent between devices are 32-bit elements; how exact they have to be, the bound alone decides.
A program may use at most 64 MiB of HBM per device.

v0:
```python
import jax
import jax.numpy as jnp
from jax import lax
from jax.sharding import PartitionSpec as P

HIGH = lax.Precision.HIGHEST


def window_pick(padded, start, relative, width):
    window = lax.dynamic_slice_in_dim(padded, start, width, 0)
    onehot = (relative[:, None] == jnp.arange(width, dtype=jnp.int32)[None, :]).astype(jnp.float32)
    return jnp.dot(onehot, window, precision=HIGH)


def per_device(
    flux,
    patch_pft,
    patch_wt,
    patch_col,
    col_wt,
    col_lu,
    lu_wt,
    lu_grid,
    cell_target,
    patch_count,
    pft_scale,
    cpl_frac,
    cpl_field,
):
    n_clump = lax.axis_size("clump")
    n_group = lax.axis_size("grp")
    n_devices = n_clump * n_group
    values = flux[0]
    patches = values.shape[0]
    width_vars = values.shape[1]
    cell_count = cell_target.shape[1]
    capacity = max(2, 2 * cell_count // n_devices)
    slot_total = n_devices * capacity
    block = min(512, patches)
    blocks = patches // block
    position = jnp.arange(patches, dtype=jnp.int32)
    alive_mask = (position < patch_count[0]).astype(jnp.float32)
    type_onehot = (
        patch_pft[0][:, None] == jnp.arange(pft_scale.shape[0], dtype=jnp.int32)[None, :]
    ).astype(jnp.float32)
    scaled = values * jnp.dot(type_onehot, pft_scale, precision=HIGH)
    col_table = jnp.stack([col_wt[0], col_lu[0].astype(jnp.float32)], axis=1)
    col_table = jnp.concatenate([col_table, jnp.zeros((block, 2), jnp.float32)], axis=0)
    lu_table = jnp.stack([lu_wt[0], lu_grid[0].astype(jnp.float32)], axis=1)
    lu_table = jnp.concatenate([lu_table, jnp.zeros((block, 2), jnp.float32)], axis=0)
    within = jnp.arange(block, dtype=jnp.int32)

    def gather_block(carry, entries):
        num_acc, den_acc = carry
        cols_blk, alive_blk, pwt_blk, scaled_blk = entries
        col_start = cols_blk[0]
        col_vals = window_pick(col_table, col_start, cols_blk - col_start, block)
        land_blk = col_vals[:, 1].astype(jnp.int32)
        land_start = land_blk[0]
        lu_vals = window_pick(lu_table, land_start, land_blk - land_start, block)
        home_blk = lu_vals[:, 1].astype(jnp.int32)
        weight_blk = alive_blk * pwt_blk * col_vals[:, 0] * lu_vals[:, 0]
        home_start = home_blk[0]
        cell_onehot = (within[:, None] == (home_blk - home_start)[None, :]).astype(jnp.float32)
        part_num = jnp.dot(cell_onehot, scaled_blk * weight_blk[:, None], precision=HIGH)
        part_den = jnp.dot(cell_onehot, weight_blk, precision=HIGH)
        old_num = lax.dynamic_slice_in_dim(num_acc, home_start, block, 0)
        old_den = lax.dynamic_slice_in_dim(den_acc, home_start, block, 0)
        num_acc = lax.dynamic_update_slice_in_dim(num_acc, old_num + part_num, home_start, 0)
        den_acc = lax.dynamic_update_slice_in_dim(den_acc, old_den + part_den, home_start, 0)
        return ((num_acc, den_acc), home_blk)

    start_acc = (
        jnp.zeros((cell_count + block, width_vars), jnp.float32),
        jnp.zeros((cell_count + block,), jnp.float32),
    )
    block_inputs = (
        patch_col[0].reshape(blocks, block),
        alive_mask.reshape(blocks, block),
        patch_wt[0].reshape(blocks, block),
        scaled.reshape(blocks, block, width_vars),
    )
    (num_acc, den_acc), home_blocks = lax.scan(gather_block, start_acc, block_inputs)
    cell_num = num_acc[:cell_count]
    cell_den = den_acc[:cell_count]
    target = cell_target[0]
    owner_dev = target // cell_count
    local_slot = target - owner_dev * cell_count
    same_owner = (owner_dev[:, None] == owner_dev[None, :]).astype(jnp.int32)
    earlier = (
        jnp.arange(cell_count, dtype=jnp.int32)[None, :]
        < jnp.arange(cell_count, dtype=jnp.int32)[:, None]
    ).astype(jnp.int32)
    rank_within = jnp.sum(same_owner * earlier, axis=1)
    slot = owner_dev * capacity + rank_within
    slot_onehot = (jnp.arange(slot_total, dtype=jnp.int32)[:, None] == slot[None, :]).astype(
        jnp.float32
    )
    slot_used = jnp.sum(slot_onehot, axis=1)
    send_slot = jnp.dot(slot_onehot, local_slot.astype(jnp.float32), precision=HIGH) + (
        1.0 - slot_used
    ) * float(cell_count)
    send_slot = send_slot.reshape(n_clump, n_group, capacity)
    cell_mean = cell_num / jnp.maximum(cell_den, 1.0)[:, None]
    send_mean = jnp.dot(slot_onehot, cell_mean, precision=HIGH)
    outgoing = (send_mean.reshape(n_clump, n_group, capacity, width_vars), send_slot)
    incoming = (
        lax.all_to_all(
            lax.all_to_all(outgoing[0], "clump", split_axis=0, concat_axis=0, tiled=True),
            "grp",
            split_axis=1,
            concat_axis=1,
            tiled=True,
        ),
        lax.all_to_all(
            lax.all_to_all(outgoing[1], "clump", split_axis=0, concat_axis=0, tiled=True),
            "grp",
            split_axis=1,
            concat_axis=1,
            tiled=True,
        ),
    )
    slot_ids = incoming[-1].reshape(-1).astype(jnp.int32)
    owner_onehot = (slot_ids[:, None] == jnp.arange(cell_count, dtype=jnp.int32)[None, :]).astype(
        jnp.float32
    )
    owned_mean = jnp.dot(owner_onehot.T, incoming[0].reshape(-1, width_vars), precision=HIGH)
    grid_merged = cpl_frac[:, None] * owned_mean + (1.0 - cpl_frac)[:, None] * cpl_field
    reply_rows = jnp.dot(owner_onehot, grid_merged, precision=HIGH).reshape(
        n_clump, n_group, capacity, width_vars
    )
    returned = lax.all_to_all(
        lax.all_to_all(reply_rows, "clump", split_axis=0, concat_axis=0, tiled=True),
        "grp",
        split_axis=1,
        concat_axis=1,
        tiled=True,
    )
    cell_merged = jnp.dot(slot_onehot.T, returned.reshape(slot_total, width_vars), precision=HIGH)
    merged_table = jnp.concatenate(
        [cell_merged, jnp.zeros((block, width_vars), jnp.float32)], axis=0
    )

    def spread_block(entries):
        home_blk, alive_blk, scaled_blk = entries
        home_start = home_blk[0]
        picked = window_pick(merged_table, home_start, home_blk - home_start, block)
        return alive_blk[:, None] * (scaled_blk - picked)

    anomaly = lax.map(
        spread_block,
        (home_blocks, alive_mask.reshape(blocks, block), scaled.reshape(blocks, block, width_vars)),
    )
    return (grid_merged, anomaly.reshape(1, patches, width_vars))


def solution(mesh):
    return jax.shard_map(
        per_device,
        mesh=mesh,
        in_specs=(
            P(("clump", "grp"), None, None),
            P(("clump", "grp"), None),
            P(("clump", "grp"), None),
            P(("clump", "grp"), None),
            P(("clump", "grp"), None),
            P(("clump", "grp"), None),
            P(("clump", "grp"), None),
            P(("clump", "grp"), None),
            P(("clump", "grp"), None),
            P(("clump", "grp")),
            P(),
            P(("clump", "grp")),
            P(("clump", "grp"), None),
        ),
        out_specs=(P(("clump", "grp"), None), P(("clump", "grp"), None, None)),
        check_vma=False,
    )
```

profile of v0, /device:TPU:0, one launch (start us, length us, event | category | flops | bytes accessed | tf_op | source)
XLA Modules:
  0.0 106.9 jit_solution(788008277498538944)
XLA Ops:
  2.6 7.4 %all-to-all-start = ((f32[8,4,8]{2,1,0:T(4,128)}), f32[8,4,8]{2,1,0:T(4,128)S(1)}, u32[]{:S(2)}, u32[]{:S(2)}) async-start(f32[8,4,8]{2,1,0:T(4,128)} %reshape.154), calls=%async_computation | async-start | bytes 32768 | tf_op jit(solution)/shard_map/all_to_all | solution.py:116
  10.1 1.5 %convolution_multiply_fusion = f32[1024,64]{0,1:T(8,128)S(1)} fusion(f32[16,64]{1,0:T(8,128)S(1)} %copy-done, f32[1,1024,64]{1,2,0:T(8,128)} %param.17, s32[1024]{0:T(1024)S(1)} %bitcast.148), kind=kOutput, calls=%fused_computation.43 | convolution fusion | flops 12664832 | bytes 532480 | tf_op jit(solution)/shard_map/dot_general | solution.py:46
  17.9 26.6 %while.26 = (s32[]{:T(128)}, f32[640,64]{0,1:T(8,128)S(1)}, f32[640]{0:T(1024)S(1)}, s32[2,512]{1,0:T(2,128)S(1)}, s32[2,512]{1,0:T(2,128)S(1)}, /*index=5*/f32[...) while((s32[]{:T(128)}, f32[640,64]{0,1:T(8,128)S(1)}, ...), condition=%wide.region_3.4_spmd.clone, body=%wide.region_2.3_spmd.clone.sunk | while | flops 218176016 | bytes 1268031 | solution.py:83
  29.6 0.8 dynamic_update_slice.24
  42.8 1.0 dynamic_update_slice.24
  44.8 0.8 reshape.183
  45.6 6.0 %all-to-all-start.2 = ((f32[8,1,2048]{2,1,0:T(1,128)}), f32[8,1,2048]{2,1,0:T(1,128)S(1)}, u32[]{:S(2)}, u32[]{:S(2)}) async-start(f32[8,1,2048]{2,1,0:T(1,128)} %reshape.183), calls=%async_computation.2 | async-start | bytes 131072 | tf_op jit(solution)/shard_map/all_to_all | solution.py:109
  52.2 6.3 %all-to-all-done.2 = f32[8,1,2048]{2,1,0:T(1,128)S(1)} async-done(((f32[8,1,2048]{2,1,0:T(1,128)}), f32[8,1,2048]{2,1,0:T(1,128)S(1)}, u32[]{:S(2)}, u32[]{:S(2)}) %all-to-all-start.2) | async-done | bytes 65568 | tf_op jit(solution)/shard_map/all_to_all | solution.py:109
  58.5 3.3 %all-to-all-start.1 = ((f32[8,4,8]{2,0,1:T(8,128)}), f32[8,4,8]{2,0,1:T(8,128)S(1)}, u32[]{:S(2)}, u32[]{:S(2)}) async-start(f32[8,4,8]{2,0,1:T(8,128)} %copy.47), calls=%async_computation.1 | async-start | bytes 32768 | tf_op jit(solution)/shard_map/all_to_all | solution.py:115
  62.3 0.8 reduce.8
  63.2 0.8 reshape.185
  64.0 1.6 %all-to-all-done.1 = f32[8,4,8]{2,0,1:T(8,128)S(1)} async-done(((f32[8,4,8]{2,0,1:T(8,128)}), f32[8,4,8]{2,0,1:T(8,128)S(1)}, u32[]{:S(2)}, u32[]{:S(2)}) %all-to-all-start.1) | async-done | bytes 1056 | tf_op jit(solution)/shard_map/all_to_all | solution.py:115
  65.6 3.3 %all-to-all-start.3 = ((f32[4,1,4096]{2,1,0:T(1,128)}), f32[4,1,4096]{2,1,0:T(1,128)S(1)}, u32[]{:S(2)}, u32[]{:S(2)}) async-start(f32[4,1,4096]{2,1,0:T(1,128)} %reshape.185), calls=%async_computation.3 | async-start | bytes 131072 | tf_op jit(solution)/shard_map/all_to_all | solution.py:108
  69.0 3.9 %all-to-all-done.3 = f32[4,1,4096]{2,1,0:T(1,128)S(1)} async-done(((f32[4,1,4096]{2,1,0:T(1,128)}), f32[4,1,4096]{2,1,0:T(1,128)S(1)}, u32[]{:S(2)}, u32[]{:S(2)}) %all-to-all-start.3) | async-done | bytes 65568 | tf_op jit(solution)/shard_map/all_to_all | solution.py:108
  72.9 0.8 reduce.9
  75.7 9.3 %all_to_all.30 = f32[8,1,2048]{2,1,0:T(1,128)S(1)} all-to-all(f32[8,1,2048]{2,1,0:T(1,128)S(1)} %reshape.187), channel_id=1, replica_groups=mesh['clump'=8,'grp'=4] {'clump'}, dimensions={0} | all-to-all | bytes 131072 | tf_op jit(solution)/shard_map/all_to_all | solution.py:133
  85.0 0.8 reduce.10
  86.6 3.3 %all-to-all-start.5 = ((f32[4,1,4096]{2,1,0:T(1,128)}), f32[4,1,4096]{2,1,0:T(1,128)S(1)}, u32[]{:S(2)}, u32[]{:S(2)}) async-start(f32[4,1,4096]{2,1,0:T(1,128)} %reshape.189), calls=%async_computation.5 | async-start | bytes 131072 | tf_op jit(solution)/shard_map/all_to_all | solution.py:132
  89.9 4.1 %all-to-all-done.5 = f32[4,1,4096]{2,1,0:T(1,128)S(1)} async-done(((f32[4,1,4096]{2,1,0:T(1,128)}), f32[4,1,4096]{2,1,0:T(1,128)S(1)}, u32[]{:S(2)}, u32[]{:S(2)}) %all-to-all-start.5) | async-done | bytes 65568 | tf_op jit(solution)/shard_map/all_to_all | solution.py:132
  94.0 0.8 reduce.11
  95.3 10.7 %while.25 = (s32[]{:T(128)}, f32[2,512,64]{1,0,2:T(2,128)S(1)}, f32[2,512]{1,0:T(2,128)S(1)}, f32[2,512,64]{1,0,2:T(2,128)S(1)}, s32[2,512]{1,0:T(2,128)S(1)}, /...) while((s32[]{:T(128)}, f32[2,512,64]{1,0,2:T(2,128)S(1)}, f32[2,512]{1,0:T(2,128)S(1)}, ...), condition=%wide.region_5.6_spmd, body=%wide.region_4.5_spmd.sunk | while | flops 201654784 | bytes 1192099 | solution.py:150
  99.4 1.2 %dynamic_update_slice.22 = f32[2,512,64]{1,0,2:T(2,128)S(1)} dynamic-update-slice(f32[2,512,64]{1,0,2:T(2,128)S(1)} %get-tuple-element.402, f32[1,512,64]{1,0,2:T(1,128)S(1)} %copy.81, s32[]{:T(128)} %get-tuple-element.401, s32[]{:T(128)} %constant.46.clone.1..sunk, s32[]{:T(128)} %constant.46.clone.1..sunk) | dynamic-update-slice | bytes 262148 | tf_op jit(solution)/shard_map/while/body/jit(dynamic_update_index_in_dim)/dynamic_update_slice | solution.py:150
  104.8 1.2 %dynamic_update_slice.22 = f32[2,512,64]{1,0,2:T(2,128)S(1)} dynamic-update-slice(f32[2,512,64]{1,0,2:T(2,128)S(1)} %get-tuple-element.402, f32[1,512,64]{1,0,2:T(1,128)S(1)} %copy.81, s32[]{:T(128)} %get-tuple-element.401, s32[]{:T(128)} %constant.46.clone.1..sunk, s32[]{:T(128)} %constant.46.clone.1..sunk) | dynamic-update-slice | bytes 262148 | tf_op jit(solution)/shard_map/while/body/jit(dynamic_update_index_in_dim)/dynamic_update_slice | solution.py:150
  106.0 0.9 reshape.160
  (117 shorter events, 29.9 us)
Async XLA Ops:
  0.6 9.4 %copy-start = (f32[16,64]{1,0:T(8,128)S(1)}, f32[16,64]{1,0:T(8,128)}, u32[]{:S(2)}) copy-start(f32[16,64]{1,0:T(8,128)} %param.27) | copy-start | bytes 12292
  0.6 0.7 copy-start.11
  2.6 7.5 %copy-start.3 = (s32[1,1024]{1,0:T(1,128)S(1)}, s32[1,1024]{1,0:T(1,128)}, u32[]{:S(2)}) copy-start(s32[1,1024]{1,0:T(1,128)} %param.18) | copy-start | bytes 12292
  2.6 42.9 %all-to-all-start = ((f32[8,4,8]{2,1,0:T(4,128)}), f32[8,4,8]{2,1,0:T(4,128)S(1)}, u32[]{:S(2)}, u32[]{:S(2)}) async-start(f32[8,4,8]{2,1,0:T(4,128)} %reshape.154), calls=%async_computation | async-start | bytes 32768 | tf_op jit(solution)/shard_map/all_to_all | solution.py:116
  12.5 0.7 copy-start.6
  13.2 0.7 copy-start.4
  14.5 0.7 copy-start.5
  15.9 0.7 copy-start.8
  16.5 0.7 copy-start.7
  17.2 0.7 copy-start.9
  45.6 12.9 %all-to-all-start.2 = ((f32[8,1,2048]{2,1,0:T(1,128)}), f32[8,1,2048]{2,1,0:T(1,128)S(1)}, u32[]{:S(2)}, u32[]{:S(2)}) async-start(f32[8,1,2048]{2,1,0:T(1,128)} %reshape.183), calls=%async_computation.2 | async-start | bytes 131072 | tf_op jit(solution)/shard_map/all_to_all | solution.py:109
  58.5 7.1 %all-to-all-start.1 = ((f32[8,4,8]{2,0,1:T(8,128)}), f32[8,4,8]{2,0,1:T(8,128)S(1)}, u32[]{:S(2)}, u32[]{:S(2)}) async-start(f32[8,4,8]{2,0,1:T(8,128)} %copy.47), calls=%async_computation.1 | async-start | bytes 32768 | tf_op jit(solution)/shard_map/all_to_all | solution.py:115
  64.0 4.9 %copy-start.10 = (f32[128]{0:T(128)S(1)}, f32[128]{0:T(128)}, u32[]{:S(2)}) copy-start(f32[128]{0:T(128)} %param.28) | copy-start | bytes 1540
  65.6 7.4 %all-to-all-start.3 = ((f32[4,1,4096]{2,1,0:T(1,128)}), f32[4,1,4096]{2,1,0:T(1,128)S(1)}, u32[]{:S(2)}, u32[]{:S(2)}) async-start(f32[4,1,4096]{2,1,0:T(1,128)} %reshape.185), calls=%async_computation.3 | async-start | bytes 131072 | tf_op jit(solution)/shard_map/all_to_all | solution.py:108
  73.9 0.8 copy-start.2
  75.0 0.6 copy-start.1
  86.6 7.4 %all-to-all-start.5 = ((f32[4,1,4096]{2,1,0:T(1,128)}), f32[4,1,4096]{2,1,0:T(1,128)S(1)}, u32[]{:S(2)}, u32[]{:S(2)}) async-start(f32[4,1,4096]{2,1,0:T(1,128)} %reshape.189), calls=%async_computation.5 | async-start | bytes 131072 | tf_op jit(solution)/shard_map/all_to_all | solution.py:132
where the time goes:
time: 108 us; the launch traced here: 107 us
  starting transfers between devices  23.3 us (22%)
  local copies, waits for them, and re-layouts  20.7 us (19%)
  waiting for transfers between devices  15.9 us (15%)
  loops' own time  15.6 us (14%)
  other arithmetic  11.2 us (10%)
  blocking collectives  9.29 us (9%)
  matrix products  9.28 us (9%)
  between operations  1.59 us (1%)
    another operation x1, loops' own time, per_device(): lax.scan(gather_block, start_acc, block_inputs)  11.6 us
    all_to_all x1, blocking collectives, per_device(): lax.all_to_all(reply_rows, 'clump', split_axis=0, concat_axis=0, tiled=True)  9.29 us
    unnamed x34, local copies, waits for them, and re-layouts  7.96 us
    all_to_all x1, starting transfers between devices, per_device(): lax.all_to_all(outgoing[1], 'clump', split_axis=0, concat_axis=0, tiled=T...  7.44 us
    all_to_all x1, waiting for transfers between devices, per_device(): lax.all_to_all(outgoing[0], 'clump', split_axis=0, concat_axis=0, tiled=T...  6.3 us
    all_to_all x1, starting transfers between devices, per_device(): lax.all_to_all(outgoing[0], 'clump', split_axis=0, concat_axis=0, tiled=T...  5.99 us
    all_to_all x1, waiting for transfers between devices, per_device(): lax.all_to_all(lax.all_to_all(reply_rows, 'clump', split_axis=0, concat_a...  4.08 us
    another operation x1, loops' own time, per_device(): lax.map(spread_block, (home_blocks, alive_mask.reshape(blocks, block), sc...  3.99 us
  transfers between devices with their start and end apart: 5, of which 4 were waited for; matrix products, arithmetic and copies ran while one was open for 22% of the time, Pallas kernels for 0%

commit v1 on v0

--- a/solution.py
+++ b/solution.py
@@ -4,6 +4,13 @@
 from jax.sharding import PartitionSpec as P
 
 HIGH = lax.Precision.HIGHEST
+
+
+def swap_blocks(block, axis, split, join):
+    count = lax.axis_size(axis)
+    blocks = jnp.stack(jnp.split(block, count, axis=split), axis=0)
+    blocks = lax.all_to_all(blocks, axis, split_axis=0, concat_axis=0)
+    return jnp.concatenate(blocks, axis=join)
 
 
 def window_pick(padded, start, relative, width):
@@ -112,12 +119,11 @@
             concat_axis=1,
             tiled=True,
         ),
-        lax.all_to_all(
+        swap_blocks(
             lax.all_to_all(outgoing[1], "clump", split_axis=0, concat_axis=0, tiled=True),
             "grp",
-            split_axis=1,
-            concat_axis=1,
-            tiled=True,
+            1,
+            1,
         ),
     )
     slot_ids = incoming[-1].reshape(-1).astype(jnp.int32)

time: 108 us -> 108 us (level)
  no operation moved by 1% of the time
where the time goes in v1:
time: 108 us; the launch traced here: 107 us
  starting transfers between devices  23.3 us (22%)
  local copies, waits for them, and re-layouts  20.3 us (19%)
  waiting for transfers between devices  16 us (15%)
  loops' own time  15.6 us (14%)
  other arithmetic  11.7 us (11%)
  blocking collectives  9.29 us (9%)
  matrix products  9.28 us (9%)
  between operations  1.59 us (1%)
    another operation x1, loops' own time, per_device(): lax.scan(gather_block, start_acc, block_inputs)  11.6 us
    all_to_all x1, blocking collectives, per_device(): lax.all_to_all(reply_rows, 'clump', split_axis=0, concat_axis=0, tiled=True)  9.29 us
    unnamed x34, local copies, waits for them, and re-layouts  7.96 us
    all_to_all x1, starting transfers between devices, per_device(): lax.all_to_all(outgoing[1], 'clump', split_axis=0, concat_axis=0, tiled=T...  7.44 us
    all_to_all x1, waiting for transfers between devices, per_device(): lax.all_to_all(outgoing[0], 'clump', split_axis=0, concat_axis=0, tiled=T...  6.28 us
    all_to_all x1, starting transfers between devices, per_device(): lax.all_to_all(outgoing[0], 'clump', split_axis=0, concat_axis=0, tiled=T...  5.99 us
    all_to_all x1, waiting for transfers between devices, per_device(): lax.all_to_all(lax.all_to_all(reply_rows, 'clump', split_axis=0, concat_a...  4.08 us
    another operation x1, loops' own time, per_device(): lax.map(spread_block, (home_blocks, alive_mask.reshape(blocks, block), sc...  3.99 us
  transfers between devices with their start and end apart: 5, of which 4 were waited for; matrix products, arithmetic and copies ran while one was open for 22% of the time, Pallas kernels for 0%

profile of v1, /device:TPU:0, one launch (start us, length us, event | category | flops | bytes accessed | tf_op | source)
XLA Modules:
  0.0 107.0 jit_solution(13205045787295517161)
XLA Ops:
  2.6 7.4 %all-to-all-start = ((f32[8,4,8]{2,1,0:T(4,128)}), f32[8,4,8]{2,1,0:T(4,128)S(1)}, u32[]{:S(2)}, u32[]{:S(2)}) async-start(f32[8,4,8]{2,1,0:T(4,128)} %reshape.154), calls=%async_computation | async-start | bytes 32768 | tf_op jit(solution)/shard_map/all_to_all | solution.py:123
  10.1 1.5 %convolution_multiply_fusion = f32[1024,64]{0,1:T(8,128)S(1)} fusion(f32[16,64]{1,0:T(8,128)S(1)} %copy-done, f32[1,1024,64]{1,2,0:T(8,128)} %param.17, s32[1024]{0:T(1024)S(1)} %bitcast.160), kind=kOutput, calls=%fused_computation.43 | convolution fusion | flops 12664832 | bytes 532480 | tf_op jit(solution)/shard_map/dot_general | solution.py:53
  17.9 26.8 %while.26 = (s32[]{:T(128)}, f32[640,64]{0,1:T(8,128)S(1)}, f32[640]{0:T(1024)S(1)}, s32[2,512]{1,0:T(2,128)S(1)}, s32[2,512]{1,0:T(2,128)S(1)}, /*index=5*/f32[...) while((s32[]{:T(128)}, f32[640,64]{0,1:T(8,128)S(1)}, ...), condition=%wide.region_3.4_spmd.clone, body=%wide.region_2.3_spmd.clone.sunk | while | flops 218176016 | bytes 1268031 | solution.py:90
  29.7 0.8 dynamic_update_slice.24
  43.0 1.0 dynamic_update_slice.24
  45.0 0.8 reshape.183
  45.7 6.0 %all-to-all-start.2 = ((f32[8,1,2048]{2,1,0:T(1,128)}), f32[8,1,2048]{2,1,0:T(1,128)S(1)}, u32[]{:S(2)}, u32[]{:S(2)}) async-start(f32[8,1,2048]{2,1,0:T(1,128)} %reshape.183), calls=%async_computation.2 | async-start | bytes 131072 | tf_op jit(solution)/shard_map/all_to_all | solution.py:116
  52.4 6.3 %all-to-all-done.2 = f32[8,1,2048]{2,1,0:T(1,128)S(1)} async-done(((f32[8,1,2048]{2,1,0:T(1,128)}), f32[8,1,2048]{2,1,0:T(1,128)S(1)}, u32[]{:S(2)}, u32[]{:S(2)}) %all-to-all-start.2) | async-done | bytes 65568 | tf_op jit(solution)/shard_map/all_to_all | solution.py:116
  58.6 3.3 %all-to-all-start.1 = ((f32[4,8,1,8]{3,1,2,0:T(8,128)}), f32[4,8,1,8]{3,1,2,0:T(8,128)S(1)}, u32[]{:S(2)}, u32[]{:S(2)}) async-start(f32[4,8,1,8]{3,1,2,0:T(8,128)} %pad_maximum_fusion), calls=%async_computation.1 | async-start | bytes 32768 | tf_op jit(solution)/shard_map/all_to_all | solution.py:12
  62.5 0.8 reduce.8
  63.3 0.8 reshape.185
  64.1 1.6 %all-to-all-done.1 = f32[4,8,1,8]{3,1,2,0:T(8,128)S(1)} async-done(((f32[4,8,1,8]{3,1,2,0:T(8,128)}), f32[4,8,1,8]{3,1,2,0:T(8,128)S(1)}, u32[]{:S(2)}, u32[]{:S(2)}) %all-to-all-start.1) | async-done | bytes 1056 | tf_op jit(solution)/shard_map/all_to_all | solution.py:12
  65.7 3.3 %all-to-all-start.3 = ((f32[4,1,4096]{2,1,0:T(1,128)}), f32[4,1,4096]{2,1,0:T(1,128)S(1)}, u32[]{:S(2)}, u32[]{:S(2)}) async-start(f32[4,1,4096]{2,1,0:T(1,128)} %reshape.185), calls=%async_computation.3 | async-start | bytes 131072 | tf_op jit(solution)/shard_map/all_to_all | solution.py:115
  69.1 4.0 %all-to-all-done.3 = f32[4,1,4096]{2,1,0:T(1,128)S(1)} async-done(((f32[4,1,4096]{2,1,0:T(1,128)}), f32[4,1,4096]{2,1,0:T(1,128)S(1)}, u32[]{:S(2)}, u32[]{:S(2)}) %all-to-all-start.3) | async-done | bytes 65568 | tf_op jit(solution)/shard_map/all_to_all | solution.py:115
  73.1 0.8 reduce.9
  75.8 9.3 %all_to_all.30 = f32[8,1,2048]{2,1,0:T(1,128)S(1)} all-to-all(f32[8,1,2048]{2,1,0:T(1,128)S(1)} %reshape.187), channel_id=1, replica_groups=mesh['clump'=8,'grp'=4] {'clump'}, dimensions={0} | all-to-all | bytes 131072 | tf_op jit(solution)/shard_map/all_to_all | solution.py:139
  85.1 0.8 reduce.10
  86.8 3.3 %all-to-all-start.5 = ((f32[4,1,4096]{2,1,0:T(1,128)}), f32[4,1,4096]{2,1,0:T(1,128)S(1)}, u32[]{:S(2)}, u32[]{:S(2)}) async-start(f32[4,1,4096]{2,1,0:T(1,128)} %reshape.189), calls=%async_computation.5 | async-start | bytes 131072 | tf_op jit(solution)/shard_map/all_to_all | solution.py:138
  90.1 4.1 %all-to-all-done.5 = f32[4,1,4096]{2,1,0:T(1,128)S(1)} async-done(((f32[4,1,4096]{2,1,0:T(1,128)}), f32[4,1,4096]{2,1,0:T(1,128)S(1)}, u32[]{:S(2)}, u32[]{:S(2)}) %all-to-all-start.5) | async-done | bytes 65568 | tf_op jit(solution)/shard_map/all_to_all | solution.py:138
  94.1 0.8 reduce.11
  95.3 10.7 %while.25 = (s32[]{:T(128)}, f32[2,512,64]{1,0,2:T(2,128)S(1)}, f32[2,512]{1,0:T(2,128)S(1)}, f32[2,512,64]{1,0,2:T(2,128)S(1)}, s32[2,512]{1,0:T(2,128)S(1)}, /...) while((s32[]{:T(128)}, f32[2,512,64]{1,0,2:T(2,128)S(1)}, f32[2,512]{1,0:T(2,128)S(1)}, ...), condition=%wide.region_5.6_spmd, body=%wide.region_4.5_spmd.sunk | while | flops 201654784 | bytes 1192099 | solution.py:156
  99.5 1.2 %dynamic_update_slice.22 = f32[2,512,64]{1,0,2:T(2,128)S(1)} dynamic-update-slice(f32[2,512,64]{1,0,2:T(2,128)S(1)} %get-tuple-element.390, f32[1,512,64]{1,0,2:T(1,128)S(1)} %copy.70, s32[]{:T(128)} %get-tuple-element.389, s32[]{:T(128)} %constant.46.clone.1..sunk, s32[]{:T(128)} %constant.46.clone.1..sunk) | dynamic-update-slice | bytes 262148 | tf_op jit(solution)/shard_map/while/body/jit(dynamic_update_index_in_dim)/dynamic_update_slice | solution.py:156
  104.8 1.2 %dynamic_update_slice.22 = f32[2,512,64]{1,0,2:T(2,128)S(1)} dynamic-update-slice(f32[2,512,64]{1,0,2:T(2,128)S(1)} %get-tuple-element.390, f32[1,512,64]{1,0,2:T(1,128)S(1)} %copy.70, s32[]{:T(128)} %get-tuple-element.389, s32[]{:T(128)} %constant.46.clone.1..sunk, s32[]{:T(128)} %constant.46.clone.1..sunk) | dynamic-update-slice | bytes 262148 | tf_op jit(solution)/shard_map/while/body/jit(dynamic_update_index_in_dim)/dynamic_update_slice | solution.py:156
  106.1 0.9 reshape.160
  (118 shorter events, 30.1 us)
Async XLA Ops:
  0.6 9.4 %copy-start = (f32[16,64]{1,0:T(8,128)S(1)}, f32[16,64]{1,0:T(8,128)}, u32[]{:S(2)}) copy-start(f32[16,64]{1,0:T(8,128)} %param.27) | copy-start | bytes 12292
  0.6 0.7 copy-start.11
  2.6 7.5 %copy-start.3 = (s32[1,1024]{1,0:T(1,128)S(1)}, s32[1,1024]{1,0:T(1,128)}, u32[]{:S(2)}) copy-start(s32[1,1024]{1,0:T(1,128)} %param.18) | copy-start | bytes 12292
  2.6 43.1 %all-to-all-start = ((f32[8,4,8]{2,1,0:T(4,128)}), f32[8,4,8]{2,1,0:T(4,128)S(1)}, u32[]{:S(2)}, u32[]{:S(2)}) async-start(f32[8,4,8]{2,1,0:T(4,128)} %reshape.154), calls=%async_computation | async-start | bytes 32768 | tf_op jit(solution)/shard_map/all_to_all | solution.py:123
  12.5 0.7 copy-start.6
  13.2 0.7 copy-start.4
  14.5 0.7 copy-start.5
  15.9 0.7 copy-start.8
  16.5 0.7 copy-start.7
  17.2 0.7 copy-start.9
  45.7 12.9 %all-to-all-start.2 = ((f32[8,1,2048]{2,1,0:T(1,128)}), f32[8,1,2048]{2,1,0:T(1,128)S(1)}, u32[]{:S(2)}, u32[]{:S(2)}) async-start(f32[8,1,2048]{2,1,0:T(1,128)} %reshape.183), calls=%async_computation.2 | async-start | bytes 131072 | tf_op jit(solution)/shard_map/all_to_all | solution.py:116
  52.4 9.5 %copy-start.10 = (f32[128]{0:T(128)S(1)}, f32[128]{0:T(128)}, u32[]{:S(2)}) copy-start(f32[128]{0:T(128)} %param.28) | copy-start | bytes 1540
  58.6 7.1 %all-to-all-start.1 = ((f32[4,8,1,8]{3,1,2,0:T(8,128)}), f32[4,8,1,8]{3,1,2,0:T(8,128)S(1)}, u32[]{:S(2)}, u32[]{:S(2)}) async-start(f32[4,8,1,8]{3,1,2,0:T(8,128)} %pad_maximum_fusion), calls=%async_computation.1 | async-start | bytes 32768 | tf_op jit(solution)/shard_map/all_to_all | solution.py:12
  65.7 7.4 %all-to-all-start.3 = ((f32[4,1,4096]{2,1,0:T(1,128)}), f32[4,1,4096]{2,1,0:T(1,128)S(1)}, u32[]{:S(2)}, u32[]{:S(2)}) async-start(f32[4,1,4096]{2,1,0:T(1,128)} %reshape.185), calls=%async_computation.3 | async-start | bytes 131072 | tf_op jit(solution)/shard_map/all_to_all | solution.py:115
  74.0 0.8 copy-start.2
  75.1 0.6 copy-start.1
  86.8 7.4 %all-to-all-start.5 = ((f32[4,1,4096]{2,1,0:T(1,128)}), f32[4,1,4096]{2,1,0:T(1,128)S(1)}, u32[]{:S(2)}, u32[]{:S(2)}) async-start(f32[4,1,4096]{2,1,0:T(1,128)} %reshape.189), calls=%async_computation.5 | async-start | bytes 131072 | tf_op jit(solution)/shard_map/all_to_all | solution.py:138
